TPU v7x, 8 devices: a whole 2x2x1 slice. The times are simulated.
8 devices in a mesh: dp: 1 (over z), tp: 8 (over y, x, core).
Axes of the slice: x: 2, y: 2, z: 1, core: 2. Of those that a mesh axis runs over, the one named last changes fastest.
Arguments:
- x_in: bfloat16 [4, 2048, 4608], P('dp', 'tp')
- positions: int32 [4, 2048], P('dp', 'tp')
- grad_out: bfloat16 [4, 2048, 4608], P('dp', 'tp')
- w_query: bfloat16 [4608, 32, 128], P(None, 'tp')
- w_key: bfloat16 [4608, 16, 128], P(None, 'tp')
- w_value: bfloat16 [4608, 16, 128], P(None, 'tp')
- w_out: bfloat16 [32, 128, 4608], P('tp')
- gain_pre: float32 [4608], replicated
- gain_post: float32 [4608], replicated
Outputs:
- output 1: bfloat16 [4, 2048, 4608], P('dp', 'tp')
- output 2: bfloat16 [4, 2048, 4608], P('dp', 'tp')
- output 3: float32 [4608, 32, 128], P('dp', 'tp')
- output 4: float32 [4608, 16, 128], P('dp', 'tp')
- output 5: float32 [4608, 16, 128], P('dp', 'tp')
- output 6: float32 [32, 128, 4608], P(('dp', 'tp'))
- output 7: float32 [4608], P('dp')
- output 8: float32 [4608], P('dp')
All inputs are finite; a program needn't handle non-finite values.
Results may differ from a plain program's by a relative error of at most 0.0177108.
Values are sent between devices in bfloat16 or wider.
A program may use at most 1 GiB of HBM per device.

v0:
```python
import jax
import jax.numpy as jnp
from jax import lax
from jax.sharding import PartitionSpec as P

WINDOW = 4096
SOFT_CAP = 50.0
NORM_EPS = 1e-6
ROPE_THETA = 10000.0


def rms_norm(hidden, scale_w):
    values = hidden.astype(jnp.float32)
    inv_rms = lax.rsqrt(jnp.mean(values * values, axis=-1, keepdims=True) + NORM_EPS)
    return (values * inv_rms * (1.0 + scale_w)).astype(jnp.bfloat16)


def rope_tables(positions, head_dim):
    half_dim = head_dim // 2
    inv_freq = ROPE_THETA ** (-2.0 * jnp.arange(half_dim, dtype=jnp.float32) / head_dim)
    angles = positions.astype(jnp.float32)[:, :, None] * inv_freq
    return jnp.cos(angles)[:, :, None, :], jnp.sin(angles)[:, :, None, :]


def apply_rope(values, cos_t, sin_t):
    half_dim = values.shape[-1] // 2
    lo_half = values[..., :half_dim]
    hi_half = values[..., half_dim:]
    return jnp.concatenate([lo_half * cos_t - hi_half * sin_t, hi_half * cos_t + lo_half * sin_t], axis=-1)


def rope_transpose(grad_in, cos_t, sin_t):
    half_dim = grad_in.shape[-1] // 2
    lo_half = grad_in[..., :half_dim]
    hi_half = grad_in[..., half_dim:]
    return jnp.concatenate([lo_half * cos_t + hi_half * sin_t, hi_half * cos_t - lo_half * sin_t], axis=-1)


def block_probs(q_blk, k_blk, pos_q, pos_k):
    scores = jnp.einsum('bqkgd,bskd->bkgqs', q_blk, k_blk, preferred_element_type=jnp.float32)
    capped = SOFT_CAP * jnp.tanh(scores / SOFT_CAP)
    pos_gap = pos_q[:, :, None] - pos_k[:, None, :]
    in_window = ((pos_gap >= 0) & (pos_gap < WINDOW))[:, None, None, :, :]
    return capped, jax.nn.softmax(jnp.where(in_window, capped, -1e30), axis=-1)


def attention_fwd(q_all, k_all, v_all, positions):
    seq_len = positions.shape[1]
    q_block = min(128, seq_len)
    slab_len = min(WINDOW + q_block, seq_len)

    def block_step(blk_idx, out_acc):
        q_start = blk_idx * q_block
        k_start = jnp.maximum(q_start + q_block - slab_len, 0)
        q_blk = lax.dynamic_slice_in_dim(q_all, q_start, q_block, axis=1)
        k_blk = lax.dynamic_slice_in_dim(k_all, k_start, slab_len, axis=1)
        v_blk = lax.dynamic_slice_in_dim(v_all, k_start, slab_len, axis=1)
        pos_q = lax.dynamic_slice_in_dim(positions, q_start, q_block, axis=1)
        pos_k = lax.dynamic_slice_in_dim(positions, k_start, slab_len, axis=1)
        prob_blk = block_probs(q_blk, k_blk, pos_q, pos_k)[1]
        out_blk = jnp.einsum('bkgqs,bskd->bqkgd', prob_blk.astype(jnp.bfloat16), v_blk, preferred_element_type=jnp.float32)
        return lax.dynamic_update_slice_in_dim(out_acc, out_blk.astype(jnp.bfloat16), q_start, axis=1)

    return lax.fori_loop(0, seq_len // q_block, block_step, jnp.zeros_like(q_all))


def attention_bwd(q_all, k_all, v_all, positions, d_out):
    seq_len = positions.shape[1]
    q_block = min(128, seq_len)
    slab_len = min(WINDOW + q_block, seq_len)

    def block_step(blk_idx, grad_acc):
        d_q, d_k, d_v = grad_acc
        q_start = blk_idx * q_block
        k_start = jnp.maximum(q_start + q_block - slab_len, 0)
        q_blk = lax.dynamic_slice_in_dim(q_all, q_start, q_block, axis=1)
        k_blk = lax.dynamic_slice_in_dim(k_all, k_start, slab_len, axis=1)
        v_blk = lax.dynamic_slice_in_dim(v_all, k_start, slab_len, axis=1)
        do_blk = lax.dynamic_slice_in_dim(d_out, q_start, q_block, axis=1)
        pos_q = lax.dynamic_slice_in_dim(positions, q_start, q_block, axis=1)
        pos_k = lax.dynamic_slice_in_dim(positions, k_start, slab_len, axis=1)
        capped, prob_blk = block_probs(q_blk, k_blk, pos_q, pos_k)
        d_prob = jnp.einsum('bqkgd,bskd->bkgqs', do_blk, v_blk, preferred_element_type=jnp.float32)
        dv_blk = jnp.einsum('bkgqs,bqkgd->bskd', prob_blk.astype(jnp.bfloat16), do_blk, preferred_element_type=jnp.float32)
        d_capped = prob_blk * (d_prob - jnp.sum(prob_blk * d_prob, axis=-1, keepdims=True))
        d_score = (d_capped * (1.0 - jnp.square(capped / SOFT_CAP))).astype(jnp.bfloat16)
        dq_blk = jnp.einsum('bkgqs,bskd->bqkgd', d_score, k_blk, preferred_element_type=jnp.float32)
        dk_blk = jnp.einsum('bkgqs,bqkgd->bskd', d_score, q_blk, preferred_element_type=jnp.float32)
        d_q = lax.dynamic_update_slice_in_dim(d_q, dq_blk, q_start, axis=1)
        d_k = lax.dynamic_update_slice_in_dim(d_k, lax.dynamic_slice_in_dim(d_k, k_start, slab_len, axis=1) + dk_blk, k_start, axis=1)
        d_v = lax.dynamic_update_slice_in_dim(d_v, lax.dynamic_slice_in_dim(d_v, k_start, slab_len, axis=1) + dv_blk, k_start, axis=1)
        return d_q, d_k, d_v

    zero_init = (jnp.zeros(q_all.shape, jnp.float32), jnp.zeros(k_all.shape, jnp.float32), jnp.zeros(v_all.shape, jnp.float32))
    return lax.fori_loop(0, seq_len // q_block, block_step, zero_init)


def solution(mesh):
    act_spec = P('dp', 'tp', None)
    head_spec = P(None, 'tp', None)
    grad_spec = P('dp', 'tp', None)
    in_specs = (act_spec, P('dp', 'tp'), act_spec, head_spec, head_spec, head_spec, P('tp', None, None), P(None), P(None))
    out_specs = (act_spec, act_spec, grad_spec, grad_spec, grad_spec, P(('dp', 'tp'), None, None), P('dp'), P('dp'))

    def local_step(x_in, positions, grad_out, w_query, w_key, w_value, w_out, gain_pre, gain_post):
        heads_loc, head_dim = w_query.shape[1], w_query.shape[2]
        kv_loc = w_key.shape[1]
        groups = heads_loc // kv_loc
        q_scale = head_dim ** -0.5
        normed, pre_pullback = jax.vjp(rms_norm, x_in, gain_pre)
        normed_all = lax.all_gather(normed, 'tp', axis=1, tiled=True)
        pos_all = lax.all_gather(positions, 'tp', axis=1, tiled=True)
        n_rows, seq_len = pos_all.shape
        cos_t, sin_t = rope_tables(pos_all, head_dim)
        q_lin = jnp.einsum('bsd,dhe->bshe', normed_all, w_query, preferred_element_type=jnp.float32)
        k_lin = jnp.einsum('bsd,dhe->bshe', normed_all, w_key, preferred_element_type=jnp.float32)
        v_lin = jnp.einsum('bsd,dhe->bshe', normed_all, w_value, preferred_element_type=jnp.float32)
        q_all = (apply_rope(q_lin, cos_t, sin_t) * q_scale).astype(jnp.bfloat16).reshape(n_rows, seq_len, kv_loc, groups, head_dim)
        k_all = apply_rope(k_lin, cos_t, sin_t).astype(jnp.bfloat16)
        v_all = v_lin.astype(jnp.bfloat16)
        attn_out = attention_fwd(q_all, k_all, v_all, pos_all).reshape(n_rows, seq_len, heads_loc, head_dim)
        part_proj = jnp.einsum('bshe,hed->bsd', attn_out, w_out, preferred_element_type=jnp.float32)
        proj_loc = lax.psum_scatter(part_proj.astype(jnp.bfloat16), 'tp', scatter_dimension=1, tiled=True)
        post_norm, post_pullback = jax.vjp(rms_norm, proj_loc, gain_post)
        y_out = (x_in.astype(jnp.float32) + post_norm.astype(jnp.float32)).astype(jnp.bfloat16)
        d_proj, d_gain_post = post_pullback(grad_out)
        d_proj_all = lax.all_gather(d_proj, 'tp', axis=1, tiled=True)
        d_attn = jnp.einsum('bsd,hed->bshe', d_proj_all, w_out, preferred_element_type=jnp.float32).astype(jnp.bfloat16)
        grad_wo = jnp.einsum('bshe,bsd->hed', attn_out, d_proj_all, preferred_element_type=jnp.float32)
        d_q, d_k, d_v = attention_bwd(q_all, k_all, v_all, pos_all, d_attn.reshape(n_rows, seq_len, kv_loc, groups, head_dim))
        dq_lin = (rope_transpose(d_q.reshape(n_rows, seq_len, heads_loc, head_dim), cos_t, sin_t) * q_scale).astype(jnp.bfloat16)
        dk_lin = rope_transpose(d_k, cos_t, sin_t).astype(jnp.bfloat16)
        dv_lin = d_v.astype(jnp.bfloat16)
        grad_wq = jnp.einsum('bsd,bshe->dhe', normed_all, dq_lin, preferred_element_type=jnp.float32)
        grad_wk = jnp.einsum('bsd,bshe->dhe', normed_all, dk_lin, preferred_element_type=jnp.float32)
        grad_wv = jnp.einsum('bsd,bshe->dhe', normed_all, dv_lin, preferred_element_type=jnp.float32)
        d_normed = (jnp.einsum('bshe,dhe->bsd', dq_lin, w_query, preferred_element_type=jnp.float32)
                    + jnp.einsum('bshe,dhe->bsd', dk_lin, w_key, preferred_element_type=jnp.float32)
                    + jnp.einsum('bshe,dhe->bsd', dv_lin, w_value, preferred_element_type=jnp.float32))
        d_normed_loc = lax.psum_scatter(d_normed.astype(jnp.bfloat16), 'tp', scatter_dimension=1, tiled=True)
        d_x_norm, d_gain_pre = pre_pullback(d_normed_loc)
        grad_x = (grad_out.astype(jnp.float32) + d_x_norm.astype(jnp.float32)).astype(jnp.bfloat16)
        grad_pre = lax.psum(d_gain_pre, 'tp')
        grad_post = lax.psum(d_gain_post, 'tp')
        return y_out, grad_x, grad_wq, grad_wk, grad_wv, grad_wo, grad_pre, grad_post

    return jax.shard_map(local_step, mesh=mesh, in_specs=in_specs, out_specs=out_specs, check_vma=False)
```

profile of v0, /device:TPU:0, one launch (start us, length us, event | category | flops | bytes accessed | tf_op | source)
XLA Modules:
  0.0 5055.1 jit_solution(18037594734621753058)
XLA Ops:
  62.4 299.8 %all-gather.3.cloned.1.call-done = bf16[4,2048,4608]{2,1,0:T(8,128)(2,1)} async-done(((bf16[4,256,4608]{2,1,0:T(8,128)(2,1)}), bf16[4,2048,4608]{2,1,0:T(8,128)(2,1)}) %all-gather.3.cloned.1.call-update) | async-done | bytes 75497488 | tf_op jit(solution)/shard_map/all_gather | solution.py:111
  362.2 32.1 fusion.102
  407.4 50.0 fusion.104
  508.7 32.0 fusion.145
  545.7 830.6 %while.33 = (s32[]{:T(128)}, bf16[4,2048,2,2,128]{4,1,3,2,0:T(8,128)(2,1)}, s32[4,2048]{1,0:T(4,128)S(1)}, bf16[4,2048,2,2,128]{4,1,3,2,0:T(8,128)(2,1)}, bf16[4...) while((s32[]{:T(128)}, ...), condition=%wide.region_4.5_spmd, body=%wide.region_1.4_spmd.sunk | while | flops 2223249408 | bytes 80795800 | solution.py:64
  1376.3 46.9 bitcast_convert_fusion
  1423.9 414.2 %reduce-scatter.3.cloned.1.call-done = bf16[4,256,4608]{2,1,0:T(8,128)(2,1)} async-done(((bf16[4,2048,4608]{2,1,0:T(8,128)(2,1)}), bf16[4,256,4608]{2,1,0:T(8,128)(2,1)}) %reduce-scatter.3.cloned.1.call-update) | async-done | bytes 9437200 | tf_op jit(solution)/shard_map/reduce_scatter | solution.py:123
  1883.0 333.7 %all-gather.5.cloned.1.call-done = bf16[4,2048,4608]{2,1,0:T(8,128)(2,1)} async-done(((bf16[4,256,4608]{2,1,0:T(8,128)(2,1)}), bf16[4,2048,4608]{2,1,0:T(8,128)(2,1)}) %all-gather.5.cloned.1.call-update) | async-done | bytes 75497488 | tf_op jit(solution)/shard_map/all_gather | solution.py:127
  2216.7 46.6 fusion.136
  2271.1 2006.5 %while.34 = (s32[]{:T(128)}, f32[4,2048,2,2,128]{1,4,3,2,0:T(8,128)}, f32[4,2048,2,128]{1,3,2,0:T(8,128)}, f32[4,2048,2,128]{1,3,2,0:T(8,128)}, s32[4,2048]{1,0:...) while((s32[]{:T(128)}, ...), condition=%wide.region_12.0_spmd.clone, body=%wide.region_8.12_spmd.clone.sunk | while | flops 5507131392 | bytes 290535648 | solution.py:95
  2327.4 29.9 fusion.223
  2357.3 32.2 bitcast_add_fusion.6
  2450.7 29.9 fusion.223
  2480.6 34.6 bitcast_add_fusion.6
  2576.3 29.9 fusion.223
  2606.2 34.6 bitcast_add_fusion.6
  2702.0 29.9 fusion.223
  2731.9 34.6 bitcast_add_fusion.6
  2827.7 29.9 fusion.223
  2857.6 34.6 bitcast_add_fusion.6
  2953.3 29.9 fusion.223
  2983.3 34.6 bitcast_add_fusion.6
  3079.0 29.9 fusion.223
  3108.9 34.6 bitcast_add_fusion.6
  3204.7 29.9 fusion.223
  3234.6 34.6 bitcast_add_fusion.6
  3330.3 29.9 fusion.223
  3360.2 34.6 bitcast_add_fusion.6
  3456.0 29.9 fusion.223
  3485.9 34.6 bitcast_add_fusion.6
  3581.6 29.9 fusion.223
  3611.5 34.6 bitcast_add_fusion.6
  3707.3 29.9 fusion.223
  3737.2 34.6 bitcast_add_fusion.6
  3833.0 29.9 fusion.223
  3862.9 34.6 bitcast_add_fusion.6
  3958.6 29.9 fusion.223
  3988.5 34.6 bitcast_add_fusion.6
  4084.3 29.9 fusion.223
  4114.2 34.6 bitcast_add_fusion.6
  4239.9 34.6 bitcast_add_fusion.6
  4294.5 52.8 %fusion.148 = f32[4,2048,4608,1]{2,1,3,0:T(8,128)} fusion(bf16[4,2048,2,64]{1,3,2,0:T(8,128)(2,1)} %get-tuple-element.439, bf16[4,2048,2,64]{1,3,2,0:T(8,128)(2,1)} %get-tuple-element.438, bf16[4608,2,128]{2,1,0:T(2,128)(2,1)} %param.17), kind=kOutput, calls=%fused_computation.163 | convolution fusion | flops 19335741440 | bytes 157548544 | tf_op jit(solution)/shard_map/bshe,dhe->bsd/dot_general | solution.py:138
  4394.4 62.2 %fusion.139 = f32[4,2048,4608,1]{2,1,3,0:T(8,128)} fusion(bf16[4608,4,128]{2,1,0:T(4,128)(2,1)} %param.16, f32[4,2048,4,64]{1,3,2,0:T(8,128)} %get-tuple-element.435, f32[4,2048,4,64]{1,3,2,0:T(8,128)} %get-tuple-element.434), kind=kOutput, calls=%fused_computation.148 | convolution fusion | flops 38667288576 | bytes 172490752 | tf_op jit(solution)/shard_map/bshe,dhe->bsd/dot_general | solution.py:137
  4456.6 121.7 %fusion.89 = bf16[4,2048,4608]{2,1,0:T(8,128)(2,1)} fusion(f32[4,2048,4608,1]{2,1,3,0:T(8,128)} %fusion.148, f32[4,2048,4608,1]{2,1,3,0:T(8,128)} %fusion.139, f32[4,2048,2,128]{1,3,2,0:T(8,128)} %get-tuple-element.342, bf16[4608,2,128]{2,1,0:T(2,128)(2,1)S(1)} %copy-done.13), kind=kOutput, calls=%fused_computation.84 | convolution fusion | flops 19442696192 | bytes 388235264 | tf_op jit(solution)/shard_map/bshe,dhe->bsd/dot_general | solution.py:139
  4578.3 50.2 fusion.127
  4644.9 30.5 fusion.133
  4691.4 48.7 fusion.124
  4740.1 253.1 %reduce-scatter.5.cloned.1.call-done = bf16[4,256,4608]{2,1,0:T(8,128)(2,1)} async-done(((bf16[4,2048,4608]{2,1,0:T(8,128)(2,1)}), bf16[4,256,4608]{2,1,0:T(8,128)(2,1)}) %reduce-scatter.5.cloned.1.call-update) | async-done | bytes 9437200 | tf_op jit(solution)/shard_map/reduce_scatter | solution.py:140
  (332 shorter events, 2164.5 us)
Async XLA Ops:
  7.2 6.2 copy-start.21
  7.2 355.0 %all-gather.3.cloned.1.call-start = ((), (), s32[]{:S(2)}) async-start(), calls=%async_computation.2 | async-start | bytes 84934656 | tf_op jit(solution)/shard_map/all_gather | solution.py:111
  12.8 0.6 copy-start.19
  13.4 0.6 copy-start.17
  14.0 0.6 copy-start.14
  25.6 0.7 copy-start.23
  25.6 15.6 copy-start.6
  25.6 1812.5 %reduce-scatter.3.cloned.1.call-start = ((), (), s32[]{:S(2)}) async-start(), calls=%async_computation.3 | async-start | bytes 84934656 | tf_op jit(solution)/shard_map/reduce_scatter | solution.py:123
  40.5 0.6 copy-start.9
  62.4 395.1 %copy-start.1 = (f32[4,2048,64]{1,2,0:T(8,128)}, f32[4,2048,64]{1,2,0:T(8,128)S(1)}, u32[]{:S(2)}) copy-start(f32[4,2048,64]{1,2,0:T(8,128)S(1)} %get-tuple-element.444) | copy-start | bytes 6291460
  362.2 32.1 copy-start.3
  493.6 15.1 copy-start.12
  508.7 37.0 copy-start.10
  1423.2 0.7 copy-start.22
  1423.2 793.5 %all-gather.5.cloned.1.call-start = ((), (), s32[]{:S(2)}) async-start(), calls=%async_computation.4 | async-start | bytes 84934656 | tf_op jit(solution)/shard_map/all_gather | solution.py:127
  1882.9 3110.3 %reduce-scatter.5.cloned.1.call-start = ((), (), s32[]{:S(2)}) async-start(), calls=%async_computation.5 | async-start | bytes 84934656 | tf_op jit(solution)/shard_map/reduce_scatter | solution.py:140
  2263.2 7.9 copy-start.11
  2271.1 2006.5 %copy-start.2 = (f32[4,2048,64]{1,2,0:T(8,128)S(1)}, f32[4,2048,64]{1,2,0:T(8,128)}, u32[]{:S(2)}) copy-start(f32[4,2048,64]{1,2,0:T(8,128)} %copy-done.1) | copy-start | bytes 6291460
  2307.0 11.3 copy-start
  2427.9 13.7 copy-start
  2553.5 13.7 copy-start
  2679.2 13.7 copy-start
  2804.9 13.7 copy-start
  2930.6 13.7 copy-start
  3056.2 13.7 copy-start
  3181.9 13.7 copy-start
  3307.5 13.7 copy-start
  3433.2 13.7 copy-start
  3558.9 13.7 copy-start
  3684.5 13.7 copy-start
  3810.2 13.7 copy-start
  3935.8 13.7 copy-start
  4061.5 13.7 copy-start
  4187.2 13.7 copy-start
  4277.6 13.8 copy-start.4
  4277.6 13.8 copy-start.8
  4294.5 52.8 %copy-start.7 = (bf16[4,2048,2,64]{1,3,2,0:T(8,128)(2,1)S(1)}, bf16[4,2048,2,64]{1,3,2,0:T(8,128)(2,1)}, u32[]{:S(2)}) copy-start(bf16[4,2048,2,64]{1,3,2,0:T(8,128)(2,1)} %get-tuple-element.438) | copy-start | bytes 6291460
  4394.4 62.2 %copy-start.13 = (bf16[4608,2,128]{2,1,0:T(2,128)(2,1)S(1)}, bf16[4608,2,128]{2,1,0:T(2,128)(2,1)}, u32[]{:S(2)}) copy-start(bf16[4608,2,128]{2,1,0:T(2,128)(2,1)} %param.18) | copy-start | bytes 7077892
  4628.5 16.4 copy-start.5
  4691.4 301.8 %copy-start.15 = (f32[4608]{0:T(1024)S(1)}, f32[4608]{0:T(1024)}, u32[]{:S(2)}) copy-start(f32[4608]{0:T(1024)} %copy-done.14) | copy-start | bytes 55300
  4691.4 301.8 %copy-start.18 = (f32[4,256]{1,0:T(4,128)S(1)}, f32[4,256]{1,0:T(4,128)}, u32[]{:S(2)}) copy-start(f32[4,256]{1,0:T(4,128)} %copy-done.17) | copy-start | bytes 12292
  4740.1 269.9 %copy-start.20 = (f32[4,256]{1,0:T(4,128)S(1)}, f32[4,256]{1,0:T(4,128)}, u32[]{:S(2)}) copy-start(f32[4,256]{1,0:T(4,128)} %copy-done.19) | copy-start | bytes 12292
  4740.1 269.9 %copy-start.16 = (f32[4608]{0:T(1024)S(1)}, f32[4608]{0:T(1024)}, u32[]{:S(2)}) copy-start(f32[4608]{0:T(1024)} %get-tuple-element.396) | copy-start | bytes 55300
Sparse Core Ops, SparseCore 0:
  25.7 336.4 all-gather.2
  1423.3 414.7 reduce-scatter.2
  1883.0 333.5 all-gather.4
  4578.5 414.7 reduce-scatter.4
where the time goes:
time: 5060 us
  matrix products  2660 us (53%)
  waiting for transfers between devices  1300 us (26%)
  other arithmetic  884 us (17%)
  local copies, waits for them, and re-layouts  153 us (3%)
    sub x32, other arithmetic, block_probs(): jax.nn.softmax(jnp.where(in_window, capped, -1e+30), axis=-1)  698 us
    dot_general x16, matrix products, block_step(): jnp.einsum('bkgqs,bqkgd->bskd', d_score, q_blk, preferred_element_type=jn...  552 us
    dot_general x16, matrix products, block_step(): jnp.einsum('bkgqs,bskd->bqkgd', d_score, k_blk, preferred_element_type=jn...  479 us
    reduce_scatter x1, waiting for transfers between devices, local_step(): lax.psum_scatter(part_proj.astype(jnp.bfloat16), 'tp', scatter_dimension=...  414 us
    dot_general x16, matrix products, block_step(): jnp.einsum('bkgqs,bskd->bqkgd', prob_blk.astype(jnp.bfloat16), v_blk, pre...  335 us
    all_gather x1, waiting for transfers between devices, local_step(): d_proj_all = lax.all_gather(d_proj, 'tp', axis=1, tiled=True)  334 us
    dot_general x32, matrix products, block_probs(): jnp.einsum('bqkgd,bskd->bkgqs', q_blk, k_blk, preferred_element_type=jnp....  334 us
    all_gather x1, waiting for transfers between devices, local_step(): normed_all = lax.all_gather(normed, 'tp', axis=1, tiled=True)  300 us
  transfers between devices with their start and end apart: 4, of which 4 were waited for; matrix products, arithmetic and copies ran while one was open for 4% of the time, Pallas kernels for 0%

commit v1 on v0

v1 whole, which is shorter than its diff:
```python
import functools

import jax
import jax.numpy as jnp
from jax import lax
from jax.experimental import pallas as pl
from jax.experimental.pallas import tpu as pltpu
from jax.sharding import PartitionSpec as P

WINDOW = 4096
SOFT_CAP = 50.0
NORM_EPS = 1e-6
ROPE_THETA = 10000.0
BLK = 256
HD = 128
CAP2 = SOFT_CAP * 1.4426950408889634


def rope_tables(positions):
    half = HD // 2
    inv_freq = ROPE_THETA ** (-2.0 * jnp.arange(half, dtype=jnp.float32) / HD)
    angles = positions.astype(jnp.float32)[:, :, None] * inv_freq
    cos, sin = jnp.cos(angles), jnp.sin(angles)
    return jnp.concatenate([cos, cos], -1), jnp.concatenate([-sin, sin], -1)


def block_tables(pos):
    rows, seq = pos.shape
    nb = seq // BLK
    blocks = pos.reshape(rows, nb, BLK)
    first, last = blocks[:, :, 0], blocks[:, :, -1]
    idx = jnp.arange(nb, dtype=jnp.int32)
    meets = (first[:, :, None] - last[:, None, :]) < WINDOW
    whole = (last[:, :, None] - first[:, None, :]) < WINDOW
    q_lo = jnp.sum(~meets, axis=2, dtype=jnp.int32)
    q_full = jnp.minimum(jnp.sum(~whole, axis=2, dtype=jnp.int32), idx)
    k_hi = jnp.sum(meets, axis=1, dtype=jnp.int32)
    k_full = jnp.maximum(jnp.sum(whole, axis=1, dtype=jnp.int32), idx + 1)
    return jnp.stack([q_lo, q_full], 1), jnp.stack([k_full, k_hi], 1)


NT = (((1,), (1,)), ((), ()))
TN = (((0,), (0,)), ((), ()))


def stack_heads(block):
    return jnp.concatenate([block[:, :HD], block[:, HD:]], axis=0)


def rope(x, cos, sin):
    return x * cos + pltpu.roll(x, HD // 2, 1) * sin


def rope_t(x, cos, sin):
    return x * cos - pltpu.roll(x, HD // 2, 1) * sin


def qkv_kernel(a_ref, w_ref, cos_ref, sin_ref, out_ref):
    cos, sin = cos_ref[...], sin_ref[...]
    for g in range(2):
        acc = jnp.dot(a_ref[...], w_ref[:, g * 512:(g + 1) * 512], preferred_element_type=jnp.float32)
        c0 = g * 512
        for h in range(2):
            q = rope(acc[:, h * HD:(h + 1) * HD], cos, sin) * (HD ** -0.5)
            out_ref[:, c0 + h * HD:c0 + (h + 1) * HD] = q.astype(jnp.bfloat16)
        out_ref[:, c0 + 256:c0 + 384] = rope(acc[:, 256:384], cos, sin).astype(jnp.bfloat16)
        out_ref[:, c0 + 384:c0 + 512] = acc[:, 384:512].astype(jnp.bfloat16)


def qkv_project(a, w, cos, sin):
    seq, dim = a.shape
    bm = 512
    return pl.pallas_call(
        qkv_kernel,
        grid=(seq // bm,),
        in_specs=[
            pl.BlockSpec((bm, dim), lambda m: (m, 0)),
            pl.BlockSpec((dim, 1024), lambda m: (0, 0)),
            pl.BlockSpec((bm, HD), lambda m: (m, 0)),
            pl.BlockSpec((bm, HD), lambda m: (m, 0)),
        ],
        out_specs=pl.BlockSpec((bm, 1024), lambda m: (m, 0)),
        out_shape=jax.ShapeDtypeStruct((seq, 1024), jnp.bfloat16),
        cost_estimate=pl.CostEstimate(flops=2 * seq * dim * 1024, bytes_accessed=2 * (seq * dim + dim * 1024 + seq * 1024), transcendentals=0),
        compiler_params=pltpu.CompilerParams(dimension_semantics=("arbitrary",), vmem_limit_bytes=60 * 1024 * 1024),
        name="qkv",
    )(a, w, cos, sin)


def fwd_kernel(tab_ref, q_ref, k_ref, v_ref, posc_ref, posr_ref, o_ref, lse_ref, acc_ref, sum_ref):
    i = pl.program_id(1)
    q = stack_heads(q_ref[...])
    acc_ref[...] = jnp.zeros_like(acc_ref)
    sum_ref[...] = jnp.zeros_like(sum_ref)

    def step(j, masked):
        r0 = pl.multiple_of(j * BLK, BLK)
        k = k_ref[pl.ds(r0, BLK), :]
        v = v_ref[pl.ds(r0, BLK), :]
        s = lax.dot_general(q, k, NT, preferred_element_type=jnp.float32)
        e = jnp.exp2(jnp.tanh(s * (1.0 / SOFT_CAP)) * CAP2)
        if masked:
            gap = posc_ref[...] - posr_ref[:, pl.ds(r0, BLK)]
            keep = (gap >= 0) & (gap < WINDOW)
            keep = jnp.concatenate([keep, keep], axis=0)
            e = jnp.where(keep, e, 0.0)
        sum_ref[...] += e[:, :HD] + e[:, HD:]
        acc_ref[...] += jnp.dot(e.astype(jnp.bfloat16), v, preferred_element_type=jnp.float32)

    lo, full = tab_ref[0, i], tab_ref[1, i]

    @pl.loop(lo, full)
    def _(j):
        step(j, True)

    @pl.loop(jnp.maximum(lo, full), i)
    def _(j):
        step(j, False)

    step(i, True)
    part = sum_ref[...]
    total = jnp.sum(part, axis=1, keepdims=True)
    o = (acc_ref[...] / total).astype(jnp.bfloat16)
    o_ref[:, :HD] = o[:BLK]
    o_ref[:, HD:] = o[BLK:]
    lse_ref[0, pl.ds(i, 1), :] = jnp.log2(jnp.sum(part.T, axis=0, keepdims=True))


def attention_fwd(qkv, tab, pos_col, pos_row):
    seq = qkv.shape[0]
    nb = seq // BLK
    grid_spec = pltpu.PrefetchScalarGridSpec(
        num_scalar_prefetch=1,
        grid=(2, nb),
        in_specs=[
            pl.BlockSpec((BLK, 256), lambda g, i, t: (i, 2 * g)),
            pl.BlockSpec((seq, HD), lambda g, i, t: (0, 4 * g + 2)),
            pl.BlockSpec((seq, HD), lambda g, i, t: (0, 4 * g + 3)),
            pl.BlockSpec((BLK, 1), lambda g, i, t: (i, 0)),
            pl.BlockSpec((1, seq), lambda g, i, t: (0, 0)),
        ],
        out_specs=[
            pl.BlockSpec((BLK, 256), lambda g, i, t: (i, g)),
            pl.BlockSpec((1, nb, 2 * BLK), lambda g, i, t: (g, 0, 0)),
        ],
        scratch_shapes=[pltpu.VMEM((2 * BLK, HD), jnp.float32), pltpu.VMEM((2 * BLK, HD), jnp.float32)],
    )
    return pl.pallas_call(
        fwd_kernel,
        grid_spec=grid_spec,
        out_shape=[jax.ShapeDtypeStruct((seq, 512), jnp.bfloat16), jax.ShapeDtypeStruct((2, nb, 2 * BLK), jnp.float32)],
        cost_estimate=pl.CostEstimate(flops=4 * seq * seq * 512, bytes_accessed=4 * seq * 1024, transcendentals=seq * seq * 4),
        compiler_params=pltpu.CompilerParams(dimension_semantics=("arbitrary", "arbitrary"), vmem_limit_bytes=48 * 1024 * 1024),
        name="attn_fwd",
    )(tab, qkv, qkv, qkv, pos_col, pos_row)


def bwd_kernel(tab_ref, q_ref, k_ref, v_ref, o_ref, do_ref, lse_ref, posc_ref, posr_ref, cos_ref, sin_ref,
               out_ref, dq_ref, dk_ref, dv_ref, delta_ref):
    j = pl.program_id(1)
    nb = pl.num_programs(1)

    @pl.when(j == 0)
    def _():
        dq_ref[...] = jnp.zeros_like(dq_ref)

        @pl.loop(0, nb)
        def _(i):
            r0 = pl.multiple_of(i * BLK, BLK)
            prod = o_ref[pl.ds(r0, BLK), :].astype(jnp.float32) * do_ref[pl.ds(r0, BLK), :].astype(jnp.float32)
            delta_ref[pl.ds(i, 1), :] = jnp.sum(stack_heads(prod).T, axis=0, keepdims=True)

    k = k_ref[...]
    v = v_ref[...]
    dk_ref[...] = jnp.zeros_like(dk_ref)
    dv_ref[...] = jnp.zeros_like(dv_ref)

    def step(i, masked):
        r0 = pl.multiple_of(i * BLK, BLK)
        q = stack_heads(q_ref[pl.ds(r0, BLK), :])
        do = stack_heads(do_ref[pl.ds(r0, BLK), :])
        s = lax.dot_general(k, q, NT, preferred_element_type=jnp.float32)
        dp = lax.dot_general(v, do, NT, preferred_element_type=jnp.float32)
        t = jnp.tanh(s * (1.0 / SOFT_CAP))
        p = jnp.exp2(t * CAP2 - lse_ref[0, pl.ds(i, 1), :])
        if masked:
            gap = posr_ref[:, pl.ds(r0, BLK)] - posc_ref[...]
            keep = (gap >= 0) & (gap < WINDOW)
            keep = jnp.concatenate([keep, keep], axis=1)
            p = jnp.where(keep, p, 0.0)
        ds = p * (dp - delta_ref[pl.ds(i, 1), :]) * (1.0 - t * t)
        pb = p.astype(jnp.bfloat16)
        dsb = ds.astype(jnp.bfloat16)
        dv_ref[...] += jnp.dot(pb, do, preferred_element_type=jnp.float32)
        dk_ref[...] += jnp.dot(dsb, q, preferred_element_type=jnp.float32)
        dq = lax.dot_general(dsb, k, TN, preferred_element_type=jnp.float32)
        dq_ref[pl.ds(r0, BLK), :HD] += dq[:BLK]
        dq_ref[pl.ds(r0, BLK), HD:] += dq[BLK:]

    full, hi = tab_ref[0, j], tab_ref[1, j]
    step(j, True)

    @pl.loop(j + 1, jnp.minimum(full, hi))
    def _(i):
        step(i, False)

    @pl.loop(full, hi)
    def _(i):
        step(i, True)

    r0 = pl.multiple_of(j * BLK, BLK)
    cos, sin = cos_ref[pl.ds(r0, BLK), :], sin_ref[pl.ds(r0, BLK), :]
    out_ref[pl.ds(r0, BLK), 256:384] = rope_t(dk_ref[...], cos, sin).astype(jnp.bfloat16)
    out_ref[pl.ds(r0, BLK), 384:512] = dv_ref[...].astype(jnp.bfloat16)

    @pl.when(j == nb - 1)
    def _():
        @pl.loop(0, nb)
        def _(i):
            s0 = pl.multiple_of(i * BLK, BLK)
            c, s = cos_ref[pl.ds(s0, BLK), :], sin_ref[pl.ds(s0, BLK), :]
            for h in range(2):
                dq = rope_t(dq_ref[pl.ds(s0, BLK), h * HD:(h + 1) * HD], c, s) * (HD ** -0.5)
                out_ref[pl.ds(s0, BLK), h * HD:(h + 1) * HD] = dq.astype(jnp.bfloat16)


def attention_bwd(qkv, o, do, lse, tab, pos_col, pos_row, cos, sin):
    seq = qkv.shape[0]
    nb = seq // BLK
    grid_spec = pltpu.PrefetchScalarGridSpec(
        num_scalar_prefetch=1,
        grid=(2, nb),
        in_specs=[
            pl.BlockSpec((seq, 256), lambda g, j, t: (0, 2 * g)),
            pl.BlockSpec((BLK, HD), lambda g, j, t: (j, 4 * g + 2)),
            pl.BlockSpec((BLK, HD), lambda g, j, t: (j, 4 * g + 3)),
            pl.BlockSpec((seq, 256), lambda g, j, t: (0, g)),
            pl.BlockSpec((seq, 256), lambda g, j, t: (0, g)),
            pl.BlockSpec((1, nb, 2 * BLK), lambda g, j, t: (g, 0, 0)),
            pl.BlockSpec((BLK, 1), lambda g, j, t: (j, 0)),
            pl.BlockSpec((1, seq), lambda g, j, t: (0, 0)),
            pl.BlockSpec((seq, HD), lambda g, j, t: (0, 0)),
            pl.BlockSpec((seq, HD), lambda g, j, t: (0, 0)),
        ],
        out_specs=pl.BlockSpec((seq, 512), lambda g, j, t: (0, g)),
        scratch_shapes=[
            pltpu.VMEM((seq, 256), jnp.float32),
            pltpu.VMEM((BLK, HD), jnp.float32),
            pltpu.VMEM((BLK, HD), jnp.float32),
            pltpu.VMEM((nb, 2 * BLK), jnp.float32),
        ],
    )
    return pl.pallas_call(
        bwd_kernel,
        grid_spec=grid_spec,
        out_shape=jax.ShapeDtypeStruct((seq, 1024), jnp.bfloat16),
        cost_estimate=pl.CostEstimate(flops=10 * seq * seq * 512, bytes_accessed=6 * seq * 1024, transcendentals=seq * seq * 4),
        compiler_params=pltpu.CompilerParams(dimension_semantics=("arbitrary", "arbitrary"), vmem_limit_bytes=48 * 1024 * 1024),
        name="attn_bwd",
    )(tab, qkv, qkv, qkv, o, do, lse, pos_col, pos_row, cos, sin)


ROW_BLK = 128


def pre_kernel(x_ref, gain_ref, out_ref):
    x = x_ref[0].astype(jnp.float32)
    inv = lax.rsqrt(jnp.mean(x * x, axis=-1, keepdims=True) + NORM_EPS)
    out_ref[...] = (x * inv * (1.0 + gain_ref[...])).astype(jnp.bfloat16)


def pre_norm(x_in, gain, b):
    _, tok, dim = x_in.shape
    return pl.pallas_call(
        pre_kernel,
        grid=(tok // ROW_BLK,),
        in_specs=[
            pl.BlockSpec((1, ROW_BLK, dim), lambda m: (b, m, 0)),
            pl.BlockSpec((1, dim), lambda m: (0, 0)),
        ],
        out_specs=pl.BlockSpec((ROW_BLK, dim), lambda m: (m, 0)),
        out_shape=jax.ShapeDtypeStruct((tok, dim), jnp.bfloat16),
        cost_estimate=pl.CostEstimate(flops=8 * tok * dim, bytes_accessed=4 * tok * dim, transcendentals=tok),
        name="pre_norm",
    )(x_in, gain)


def fold_rows(x):
    return jnp.sum(x.reshape(x.shape[0] // 8, 8, x.shape[1]), axis=0)


def rms_bwd(u, g, gain):
    inv = lax.rsqrt(jnp.mean(u * u, axis=-1, keepdims=True) + NORM_EPS)
    normed = u * inv
    d_gain = fold_rows(g * normed)
    h = g * (1.0 + gain)
    d_u = inv * (h - normed * jnp.mean(h * normed, axis=-1, keepdims=True))
    return d_u, d_gain


def post_kernel(n_parts, has_prev, *refs):
    parts, (x_ref, g_ref, gain_ref) = refs[:n_parts], refs[n_parts:n_parts + 3]
    y_ref, dr_ref, dgain_ref = refs[-3:]
    r = parts[0][...].astype(jnp.float32)
    for p in parts[1:]:
        r = (r + p[...].astype(jnp.float32))
    r = r.astype(jnp.bfloat16).astype(jnp.float32)
    gain = gain_ref[...]
    g = g_ref[0].astype(jnp.float32)
    inv = lax.rsqrt(jnp.mean(r * r, axis=-1, keepdims=True) + NORM_EPS)
    post = (r * inv * (1.0 + gain)).astype(jnp.bfloat16)
    y_ref[0] = (x_ref[0].astype(jnp.float32) + post.astype(jnp.float32)).astype(jnp.bfloat16)
    d_r, d_gain = rms_bwd(r, g, gain)
    dr_ref[...] = d_r.astype(jnp.bfloat16)

    @pl.when(pl.program_id(0) == 0)
    def _():
        dgain_ref[...] = jnp.zeros_like(dgain_ref)

    dgain_ref[...] += d_gain


def final_kernel(n_parts, has_prev, *refs):
    parts, (x_ref, g_ref, gain_ref) = refs[:n_parts], refs[n_parts:n_parts + 3]
    gx_ref, dgain_ref = refs[-2:]
    da = parts[0][...].astype(jnp.float32)
    for p in parts[1:]:
        da = (da + p[...].astype(jnp.float32))
    da = da.astype(jnp.bfloat16).astype(jnp.float32)
    d_x, d_gain = rms_bwd(x_ref[0].astype(jnp.float32), da, gain_ref[...])
    d_x = d_x.astype(jnp.bfloat16).astype(jnp.float32)
    gx_ref[0] = (g_ref[0].astype(jnp.float32) + d_x).astype(jnp.bfloat16)

    @pl.when(pl.program_id(0) == 0)
    def _():
        dgain_ref[...] = jnp.zeros_like(dgain_ref)

    dgain_ref[...] += d_gain


def token_stage(kernel, name, parts, x_in, grad_out, gain, b, prev, with_dr):
    n_rows, tok, dim = x_in.shape
    blk = pl.BlockSpec((ROW_BLK, dim), lambda m: (m, 0))
    row = pl.BlockSpec((1, ROW_BLK, dim), lambda m: (b, m, 0))
    args = [*parts, x_in, grad_out, gain]
    in_specs = [blk] * len(parts) + [row, row, pl.BlockSpec((1, dim), lambda m: (0, 0))]
    alias = {}
    if prev is not None:
        alias = {len(args): 0}
        args.append(prev)
        in_specs.append(pl.BlockSpec(memory_space=pl.ANY))
    out_shape = [jax.ShapeDtypeStruct(x_in.shape, jnp.bfloat16)]
    out_specs = [row]
    if with_dr:
        out_shape.append(jax.ShapeDtypeStruct((tok, dim), jnp.bfloat16))
        out_specs.append(blk)
    out_shape.append(jax.ShapeDtypeStruct((8, dim), jnp.float32))
    out_specs.append(pl.BlockSpec((8, dim), lambda m: (0, 0)))
    return pl.pallas_call(
        functools.partial(kernel, len(parts), prev is not None),
        grid=(tok // ROW_BLK,),
        in_specs=in_specs,
        out_specs=out_specs,
        out_shape=out_shape,
        input_output_aliases=alias,
        cost_estimate=pl.CostEstimate(flops=30 * tok * dim, bytes_accessed=10 * tok * dim, transcendentals=tok),
        compiler_params=pltpu.CompilerParams(dimension_semantics=("arbitrary",), vmem_limit_bytes=40 * 1024 * 1024),
        name=name,
    )(*args)


def solution(mesh):
    act_spec = P('dp', 'tp', None)
    head_spec = P(None, 'tp', None)
    grad_spec = P('dp', 'tp', None)
    in_specs = (act_spec, P('dp', 'tp'), act_spec, head_spec, head_spec, head_spec, P('tp', None, None), P(None), P(None))
    out_specs = (act_spec, act_spec, grad_spec, grad_spec, grad_spec, P(('dp', 'tp'), None, None), P('dp'), P('dp'))
    f32 = jnp.float32

    def local_step(x_in, positions, grad_out, w_query, w_key, w_value, w_out, gain_pre, gain_post):
        n_rows, dim = x_in.shape[0], x_in.shape[2]
        rows = range(n_rows)
        w_o = w_out.reshape(512, dim)
        w_qkv = jnp.concatenate(
            [w_query[:, 0], w_query[:, 1], w_key[:, 0], w_value[:, 0], w_query[:, 2], w_query[:, 3], w_key[:, 1], w_value[:, 1]], axis=1)

        gain_pre2, gain_post2 = gain_pre[None, :], gain_post[None, :]
        normed = [lax.all_gather(pre_norm(x_in, gain_pre2, b), 'tp', axis=0, tiled=True) for b in rows]
        pos = lax.all_gather(positions, 'tp', axis=1, tiled=True)
        cos, sin = rope_tables(pos)
        q_tab, k_tab = block_tables(pos)

        qkv, o, lse, dqkv, dr = {}, {}, {}, {}, {}
        y_out, grad_x = None, None
        g_post, g_pre = [], []
        g_wo = None
        for b in rows:
            pos_col, pos_row = pos[b][:, None], pos[b][None, :]
            qkv[b] = qkv_project(normed[b], w_qkv, cos[b], sin[b])
            o[b], lse[b] = attention_fwd(qkv[b], q_tab[b], pos_col, pos_row)
            part = jnp.dot(o[b], w_o, preferred_element_type=f32).astype(jnp.bfloat16)
            proj = lax.psum_scatter(part, 'tp', scatter_dimension=0, tiled=True)
            y_out, d_proj, d_gain = token_stage(post_kernel, "post_norm", [proj], x_in, grad_out, gain_post2, b, y_out, True)
            g_post.append(d_gain)
            dr[b] = lax.all_gather(d_proj, 'tp', axis=0, tiled=True)
        for b in rows:
            pos_col, pos_row = pos[b][:, None], pos[b][None, :]
            d_attn = lax.dot_general(dr[b], w_o, NT, preferred_element_type=f32).astype(jnp.bfloat16)
            dqkv[b] = attention_bwd(qkv[b], o[b], d_attn, lse[b], k_tab[b], pos_col, pos_row, cos[b], sin[b])
            d_a = lax.dot_general(dqkv[b], w_qkv, NT, preferred_element_type=f32).astype(jnp.bfloat16)
            d_a_loc = lax.psum_scatter(d_a, 'tp', scatter_dimension=0, tiled=True)
            grad_x, d_gain = token_stage(final_kernel, "pre_norm_bwd", [d_a_loc], x_in, grad_out, gain_pre2, b, grad_x, False)
            g_pre.append(d_gain)
        g_w = None
        for b in rows:
            t = lax.dot_general(o[b], dr[b], TN, preferred_element_type=f32)
            g_wo = t if g_wo is None else g_wo + t
            t = lax.dot_general(normed[b], dqkv[b], TN, preferred_element_type=f32)
            g_w = t if g_w is None else g_w + t
        grad_wq = jnp.stack([g_w[:, 0:128], g_w[:, 128:256], g_w[:, 512:640], g_w[:, 640:768]], axis=1)
        grad_wk = jnp.stack([g_w[:, 256:384], g_w[:, 768:896]], axis=1)
        grad_wv = jnp.stack([g_w[:, 384:512], g_w[:, 896:1024]], axis=1)
        grad_wo = g_wo.reshape(4, 128, dim)
        grad_pre = lax.psum(jnp.sum(sum(g_pre), axis=0), 'tp')
        grad_post = lax.psum(jnp.sum(sum(g_post), axis=0), 'tp')
        return y_out, grad_x, grad_wq, grad_wk, grad_wv, grad_wo, grad_pre, grad_post

    return jax.shard_map(local_step, mesh=mesh, in_specs=in_specs, out_specs=out_specs, check_vma=False)
```

time: 5060 us -> 1790 us (0.35)
  matrix products: 2660 us -> 419 us
  other arithmetic: 884 us -> 25.1 us
  waiting for transfers between devices: 1300 us -> 684 us
  Pallas kernels: 0 us -> 453 us
    dot_general x124 -> x20, matrix products: 2660 us -> 419 us  [the longest x4 114 us: local_step(): t = lax.dot_general(normed[b], dqkv[b], TN, preferred_element_type=f32)]
    sub x33 -> x0, other arithmetic: 710 us -> none  [the longest x32 698 us: block_probs(): jax.nn.softmax(jnp.where(in_window, capped, -1e+30), axis=-1)]
    pallas_call x0 -> x24, Pallas kernels: none -> 453 us  [the longest x4 170 us: attention_bwd(): pl.pallas_call(bwd_kernel, grid_spec=grid_spec, out_shape=jax.ShapeDtypeS...]
    all_gather x2 -> x8, waiting for transfers between devices: 633 us -> 231 us  [the longest x4 122 us: local_step(): dr[b] = lax.all_gather(d_proj, 'tp', axis=0, tiled=True)]
    reduce_scatter x2 -> x8, waiting for transfers between devices: 667 us -> 452 us  [the longest x4 363 us: local_step(): proj = lax.psum_scatter(part, 'tp', scatter_dimension=0, tiled=True)]
    convert_element_type x4 -> x0, other arithmetic: 62.4 us -> none  [the longest x1 21.6 us: rms_norm(): values = hidden.astype(jnp.float32)]
    unnamed x51 -> x167, local copies, waits for them, and re-layouts: 67.1 us -> 119 us
  transfers between devices with their start and end apart: 4 -> 16, of which waited for: 4 -> 13; matrix products, arithmetic and copies ran while one was open for 4% -> 30% of each run, Pallas kernels for 0% -> 25%
where the time goes in v1:
time: 1790 us; the launch traced here: 1780 us
  waiting for transfers between devices  684 us (38%)
  Pallas kernels  453 us (25%)
  matrix products  419 us (23%)
  local copies, waits for them, and re-layouts  147 us (8%)
  blocking collectives  37.8 us (2%)
  other arithmetic  25.1 us (1%)
    reduce_scatter x4, waiting for transfers between devices, local_step(): proj = lax.psum_scatter(part, 'tp', scatter_dimension=0, tiled=True)  363 us
    pallas_call x4, Pallas kernels, attention_bwd(): pl.pallas_call(bwd_kernel, grid_spec=grid_spec, out_shape=jax.ShapeDtypeS...  170 us
    all_gather x4, waiting for transfers between devices, local_step(): dr[b] = lax.all_gather(d_proj, 'tp', axis=0, tiled=True)  122 us
    unnamed x167, local copies, waits for them, and re-layouts  119 us
    dot_general x4, matrix products, local_step(): t = lax.dot_general(normed[b], dqkv[b], TN, preferred_element_type=f32)  114 us
    all_gather x4, waiting for transfers between devices, local_step(): lax.all_gather(pre_norm(x_in, gain_pre2, b), 'tp', axis=0, tiled=True)  110 us
    pallas_call x4, Pallas kernels, qkv_project(): pl.pallas_call(qkv_kernel, grid=(seq // bm,), in_specs=[pl.BlockSpec((bm,...  109 us
    dot_general x4, matrix products, local_step(): lax.dot_general(dqkv[b], w_qkv, NT, preferred_element_type=f32)  104 us
  transfers between devices with their start and end apart: 16, of which 13 were waited for; matrix products, arithmetic and copies ran while one was open for 30% of the time, Pallas kernels for 25%

profile of v1, /device:TPU:0, one launch (start us, length us, event | category | flops | bytes accessed | tf_op | source)
XLA Modules:
  0.0 1780.7 jit_solution(12647486600505812225)
XLA Ops:
  40.7 14.9 multiply_sine_fusion
  83.3 25.6 %all-gather.15.cloned.1.call-done.a_ref = bf16[2048,4608]{1,0:T(8,128)(2,1)} async-done(((bf16[256,4608]{1,0:T(8,128)(2,1)}), bf16[2048,4608]{1,0:T(8,128)(2,1)}) %all-gather.15.cloned.1.call-update) | async-done | bytes 18874384 | tf_op jit(solution)/shard_map/all_gather | solution.py:388
  108.9 27.1 %qkv.7.q_ref.k_ref.v_ref = bf16[2048,1024]{1,0:T(8,128)(2,1)} custom-call(bf16[2048,4608]{1,0:T(8,128)(2,1)} %all-gather.15.cloned.1.call-done.a_ref, bf16[4608,1024]{1,0:T(8,128)(2,1)} %fusion.1.w_ref, f32[2048,128]{1,0:T(8,128)} %get-tuple-element.144.cos_ref, f32[2048,128]{1,0:T(8,128)} %get-tuple-element.102.sin_ref), custom_call_target="tpu_custom_call" | custom-call | flops 19327352832 | bytes 32505856 | tf_op jit(solution)/shard_map/qkv/pallas_call | solution.py:73
  136.0 20.7 %attn_fwd.7 = (bf16[2048,512]{1,0:T(8,128)(2,1)S(1)}, f32[2,8,512]{2,1,0:T(8,128)S(1)}) custom-call(s32[2,8]{1,0:T(2,128)S(1)} %bitcast.138, bf16[2048,1024]{1,0:T(8,128)(2,1)} %qkv.7.q_ref.k_ref.v_ref, bf16[2048,1024]{1,0:T(8,128)(2,1)} %qkv.7.q_ref.k_ref.v_ref, bf16[2048,1024]{1,0:T(8,128)(2,1)} %qkv.7.q_ref.k_ref.v_ref, s32[2048,1]{1,0:T(8,128)S(1)} %copy.70.posc_ref, ...), custom_call_target="tpu_custom_call" | custom-call | flops 8589934592 | bytes 8388608 | tf_op jit(solution)/shard_map/attn_fwd/pallas_call | solution.py:148
  157.2 15.4 convolution_convert_fusion
  174.4 29.8 %all-gather.13.cloned.1.call-done.a_ref = bf16[2048,4608]{1,0:T(8,128)(2,1)} async-done(((bf16[256,4608]{1,0:T(8,128)(2,1)}), bf16[2048,4608]{1,0:T(8,128)(2,1)}) %all-gather.13.cloned.1.call-update) | async-done | bytes 18874384 | tf_op jit(solution)/shard_map/all_gather | solution.py:388
  204.3 27.3 %qkv.6.q_ref.k_ref.v_ref = bf16[2048,1024]{1,0:T(8,128)(2,1)} custom-call(bf16[2048,4608]{1,0:T(8,128)(2,1)} %all-gather.13.cloned.1.call-done.a_ref, bf16[4608,1024]{1,0:T(8,128)(2,1)} %fusion.1.w_ref, f32[2048,128]{1,0:T(8,128)} %get-tuple-element.142.cos_ref, f32[2048,128]{1,0:T(8,128)} %get-tuple-element.104.sin_ref), custom_call_target="tpu_custom_call" | custom-call | flops 19327352832 | bytes 32505856 | tf_op jit(solution)/shard_map/qkv/pallas_call | solution.py:73
  231.6 24.1 %attn_fwd.6 = (bf16[2048,512]{1,0:T(8,128)(2,1)S(1)}, f32[2,8,512]{2,1,0:T(8,128)S(1)}) custom-call(s32[2,8]{1,0:T(2,128)S(1)} %bitcast.137, bf16[2048,1024]{1,0:T(8,128)(2,1)} %qkv.6.q_ref.k_ref.v_ref, bf16[2048,1024]{1,0:T(8,128)(2,1)} %qkv.6.q_ref.k_ref.v_ref, bf16[2048,1024]{1,0:T(8,128)(2,1)} %qkv.6.q_ref.k_ref.v_ref, s32[2048,1]{1,0:T(8,128)S(1)} %copy.69.posc_ref, ...), custom_call_target="tpu_custom_call" | custom-call | flops 8589934592 | bytes 8388608 | tf_op jit(solution)/shard_map/attn_fwd/pallas_call | solution.py:148
  256.3 15.5 convolution_convert_fusion.1
  273.5 26.1 %all-gather.11.cloned.1.call-done.a_ref = bf16[2048,4608]{1,0:T(8,128)(2,1)} async-done(((bf16[256,4608]{1,0:T(8,128)(2,1)}), bf16[2048,4608]{1,0:T(8,128)(2,1)}) %all-gather.11.cloned.1.call-update) | async-done | bytes 18874384 | tf_op jit(solution)/shard_map/all_gather | solution.py:388
  299.6 27.5 %qkv.5.q_ref.k_ref.v_ref = bf16[2048,1024]{1,0:T(8,128)(2,1)} custom-call(bf16[2048,4608]{1,0:T(8,128)(2,1)} %all-gather.11.cloned.1.call-done.a_ref, bf16[4608,1024]{1,0:T(8,128)(2,1)} %fusion.1.w_ref, f32[2048,128]{1,0:T(8,128)} %get-tuple-element.143.cos_ref, f32[2048,128]{1,0:T(8,128)} %get-tuple-element.103.sin_ref), custom_call_target="tpu_custom_call" | custom-call | flops 19327352832 | bytes 32505856 | tf_op jit(solution)/shard_map/qkv/pallas_call | solution.py:73
  327.2 21.6 %attn_fwd.5 = (bf16[2048,512]{1,0:T(8,128)(2,1)S(1)}, f32[2,8,512]{2,1,0:T(8,128)S(1)}) custom-call(s32[2,8]{1,0:T(2,128)S(1)} %bitcast.135, bf16[2048,1024]{1,0:T(8,128)(2,1)} %qkv.5.q_ref.k_ref.v_ref, bf16[2048,1024]{1,0:T(8,128)(2,1)} %qkv.5.q_ref.k_ref.v_ref, bf16[2048,1024]{1,0:T(8,128)(2,1)} %qkv.5.q_ref.k_ref.v_ref, s32[2048,1]{1,0:T(8,128)S(1)} %copy.68.posc_ref, ...), custom_call_target="tpu_custom_call" | custom-call | flops 8589934592 | bytes 8388608 | tf_op jit(solution)/shard_map/attn_fwd/pallas_call | solution.py:148
  348.8 15.5 convolution_convert_fusion.2
  366.6 28.3 %all-gather.9.cloned.1.call-done.a_ref = bf16[2048,4608]{1,0:T(8,128)(2,1)} async-done(((bf16[256,4608]{1,0:T(8,128)(2,1)}), bf16[2048,4608]{1,0:T(8,128)(2,1)}) %all-gather.9.cloned.1.call-update) | async-done | bytes 18874384 | tf_op jit(solution)/shard_map/all_gather | solution.py:388
  394.9 27.2 %qkv.4.q_ref.k_ref.v_ref = bf16[2048,1024]{1,0:T(8,128)(2,1)} custom-call(bf16[2048,4608]{1,0:T(8,128)(2,1)} %all-gather.9.cloned.1.call-done.a_ref, bf16[4608,1024]{1,0:T(8,128)(2,1)} %fusion.1.w_ref, f32[2048,128]{1,0:T(8,128)} %get-tuple-element.141.cos_ref, f32[2048,128]{1,0:T(8,128)} %get-tuple-element.105.sin_ref), custom_call_target="tpu_custom_call" | custom-call | flops 19327352832 | bytes 32505856 | tf_op jit(solution)/shard_map/qkv/pallas_call | solution.py:73
  422.2 35.4 %attn_fwd.4 = (bf16[2048,512]{1,0:T(8,128)(2,1)S(1)}, f32[2,8,512]{2,1,0:T(8,128)S(1)}) custom-call(s32[2,8]{1,0:T(2,128)S(1)} %bitcast.134, bf16[2048,1024]{1,0:T(8,128)(2,1)} %qkv.4.q_ref.k_ref.v_ref, bf16[2048,1024]{1,0:T(8,128)(2,1)} %qkv.4.q_ref.k_ref.v_ref, bf16[2048,1024]{1,0:T(8,128)(2,1)} %qkv.4.q_ref.k_ref.v_ref, s32[2048,1]{1,0:T(8,128)S(1)} %copy.67.posc_ref, ...), custom_call_target="tpu_custom_call" | custom-call | flops 8589934592 | bytes 8388608 | tf_op jit(solution)/shard_map/attn_fwd/pallas_call | solution.py:148
  457.6 15.4 convolution_convert_fusion.3
  475.1 40.3 %reduce-scatter.15.cloned.1.call-done.refs_0_ = bf16[256,4608]{1,0:T(8,128)(2,1)} async-done(((bf16[2048,4608]{1,0:T(8,128)(2,1)}), bf16[256,4608]{1,0:T(8,128)(2,1)}) %reduce-scatter.15.cloned.1.call-update) | async-done | bytes 2359312 | tf_op jit(solution)/shard_map/reduce_scatter | solution.py:402
  528.2 107.6 %reduce-scatter.13.cloned.1.call-done.refs_0_ = bf16[256,4608]{1,0:T(8,128)(2,1)} async-done(((bf16[2048,4608]{1,0:T(8,128)(2,1)}), bf16[256,4608]{1,0:T(8,128)(2,1)}) %reduce-scatter.13.cloned.1.call-update) | async-done | bytes 2359312 | tf_op jit(solution)/shard_map/reduce_scatter | solution.py:402
  649.0 107.5 %reduce-scatter.11.cloned.1.call-done.refs_0_ = bf16[256,4608]{1,0:T(8,128)(2,1)} async-done(((bf16[2048,4608]{1,0:T(8,128)(2,1)}), bf16[256,4608]{1,0:T(8,128)(2,1)}) %reduce-scatter.11.cloned.1.call-update) | async-done | bytes 2359312 | tf_op jit(solution)/shard_map/reduce_scatter | solution.py:402
  769.4 107.8 %reduce-scatter.9.cloned.1.call-done.refs_0_ = bf16[256,4608]{1,0:T(8,128)(2,1)} async-done(((bf16[2048,4608]{1,0:T(8,128)(2,1)}), bf16[256,4608]{1,0:T(8,128)(2,1)}) %reduce-scatter.9.cloned.1.call-update) | async-done | bytes 2359312 | tf_op jit(solution)/shard_map/reduce_scatter | solution.py:402
  890.6 81.3 %all-gather.23.cloned.1.call-done = bf16[2048,4608]{1,0:T(8,128)(2,1)} async-done(((bf16[256,4608]{1,0:T(8,128)(2,1)}), bf16[2048,4608]{1,0:T(8,128)(2,1)}) %all-gather.23.cloned.1.call-update) | async-done | bytes 18874384 | tf_op jit(solution)/shard_map/all_gather | solution.py:405
  971.9 16.7 convolution_convert_fusion.8.do_ref
  988.7 35.6 %attn_bwd.7 = bf16[2048,1024]{1,0:T(8,128)(2,1)} custom-call(s32[2,8]{1,0:T(2,128)S(1)} %bitcast.141, bf16[2048,1024]{1,0:T(8,128)(2,1)} %qkv.7.q_ref.k_ref.v_ref, bf16[2048,1024]{1,0:T(8,128)(2,1)} %qkv.7.q_ref.k_ref.v_ref, bf16[2048,1024]{1,0:T(8,128)(2,1)} %qkv.7.q_ref.k_ref.v_ref, bf16[2048,512]{1,0:T(8,128)(2,1)S(1)} %copy-done.48, ...), custom_call_target="tpu_custom_call" | custom-call | flops 21474836480 | bytes 12582912 | tf_op jit(solution)/shard_map/attn_bwd/pallas_call | solution.py:253
  1024.2 26.2 %convolution_convert_fusion.4 = bf16[2048,4608]{1,0:T(8,128)(2,1)} fusion(bf16[2048,1024]{1,0:T(8,128)(2,1)} %attn_bwd.7, bf16[4608,1024]{1,0:T(8,128)(2,1)} %fusion.1.w_ref), kind=kOutput, calls=%fused_computation.4 | convolution fusion | flops 19336790016 | bytes 32505856 | tf_op jit(solution)/shard_map/dot_general | solution.py:410
  1050.5 16.1 all-gather.21.cloned.1.call-done
  1066.6 16.4 convolution_convert_fusion.9.do_ref
  1083.8 40.7 %attn_bwd.6 = bf16[2048,1024]{1,0:T(8,128)(2,1)} custom-call(s32[2,8]{1,0:T(2,128)S(1)} %bitcast.140, bf16[2048,1024]{1,0:T(8,128)(2,1)} %qkv.6.q_ref.k_ref.v_ref, bf16[2048,1024]{1,0:T(8,128)(2,1)} %qkv.6.q_ref.k_ref.v_ref, bf16[2048,1024]{1,0:T(8,128)(2,1)} %qkv.6.q_ref.k_ref.v_ref, bf16[2048,512]{1,0:T(8,128)(2,1)S(1)} %copy-done.51, ...), custom_call_target="tpu_custom_call" | custom-call | flops 21474836480 | bytes 12582912 | tf_op jit(solution)/shard_map/attn_bwd/pallas_call | solution.py:253
  1124.5 26.2 %convolution_convert_fusion.5 = bf16[2048,4608]{1,0:T(8,128)(2,1)} fusion(bf16[2048,1024]{1,0:T(8,128)(2,1)} %attn_bwd.6, bf16[4608,1024]{1,0:T(8,128)(2,1)} %fusion.1.w_ref), kind=kOutput, calls=%fused_computation.5 | convolution fusion | flops 19336790016 | bytes 32505856 | tf_op jit(solution)/shard_map/dot_general | solution.py:410
  1161.5 16.4 convolution_convert_fusion.10.do_ref
  1177.9 37.0 %attn_bwd.5 = bf16[2048,1024]{1,0:T(8,128)(2,1)} custom-call(s32[2,8]{1,0:T(2,128)S(1)} %bitcast.139, bf16[2048,1024]{1,0:T(8,128)(2,1)} %qkv.5.q_ref.k_ref.v_ref, bf16[2048,1024]{1,0:T(8,128)(2,1)} %qkv.5.q_ref.k_ref.v_ref, bf16[2048,1024]{1,0:T(8,128)(2,1)} %qkv.5.q_ref.k_ref.v_ref, bf16[2048,512]{1,0:T(8,128)(2,1)S(1)} %copy-done.54, ...), custom_call_target="tpu_custom_call" | custom-call | flops 21474836480 | bytes 12582912 | tf_op jit(solution)/shard_map/attn_bwd/pallas_call | solution.py:253
  1214.9 26.1 %convolution_convert_fusion.6 = bf16[2048,4608]{1,0:T(8,128)(2,1)} fusion(bf16[2048,1024]{1,0:T(8,128)(2,1)} %attn_bwd.5, bf16[4608,1024]{1,0:T(8,128)(2,1)} %fusion.1.w_ref), kind=kOutput, calls=%fused_computation.6 | convolution fusion | flops 19336790016 | bytes 32505856 | tf_op jit(solution)/shard_map/dot_general | solution.py:410
  1256.2 16.7 convolution_convert_fusion.11.do_ref
  1272.9 56.6 %attn_bwd.4 = bf16[2048,1024]{1,0:T(8,128)(2,1)} custom-call(s32[2,8]{1,0:T(2,128)S(1)} %bitcast.136, bf16[2048,1024]{1,0:T(8,128)(2,1)} %qkv.4.q_ref.k_ref.v_ref, bf16[2048,1024]{1,0:T(8,128)(2,1)} %qkv.4.q_ref.k_ref.v_ref, bf16[2048,1024]{1,0:T(8,128)(2,1)} %qkv.4.q_ref.k_ref.v_ref, bf16[2048,512]{1,0:T(8,128)(2,1)S(1)} %copy-done.9, ...), custom_call_target="tpu_custom_call" | custom-call | flops 21474836480 | bytes 12582912 | tf_op jit(solution)/shard_map/attn_bwd/pallas_call | solution.py:253
  1329.5 26.1 %convolution_convert_fusion.7 = bf16[2048,4608]{1,0:T(8,128)(2,1)} fusion(bf16[2048,1024]{1,0:T(8,128)(2,1)} %attn_bwd.4, bf16[4608,1024]{1,0:T(8,128)(2,1)} %fusion.1.w_ref), kind=kOutput, calls=%fused_computation.7 | convolution fusion | flops 19336790016 | bytes 32505856 | tf_op jit(solution)/shard_map/dot_general | solution.py:410
  1355.6 26.5 %fusion.38 = f32[4608,1024]{1,0:T(8,128)} fusion(bf16[2048,4608]{1,0:T(8,128)(2,1)} %all-gather.11.cloned.1.call-done.a_ref, bf16[2048,1024]{1,0:T(8,128)(2,1)} %attn_bwd.5), kind=kOutput, calls=%fused_computation.118 | convolution fusion | flops 19327352832 | bytes 41943040 | tf_op jit(solution)/shard_map/dot_general | solution.py:418
  1382.1 25.4 %fusion.37 = f32[4608,1024]{1,0:T(8,128)} fusion(bf16[2048,4608]{1,0:T(8,128)(2,1)} %all-gather.13.cloned.1.call-done.a_ref, bf16[2048,1024]{1,0:T(8,128)(2,1)S(1)} %copy-done.69), kind=kOutput, calls=%fused_computation.117 | convolution fusion | flops 19327352832 | bytes 41943040 | tf_op jit(solution)/shard_map/dot_general | solution.py:418
  1407.6 23.3 %fusion.36 = f32[4608,1024]{1,0:T(8,128)} fusion(bf16[2048,4608]{1,0:T(8,128)(2,1)S(1)} %bitcast.152, bf16[2048,1024]{1,0:T(8,128)(2,1)S(1)} %copy-done.68), kind=kOutput, calls=%fused_computation.116 | convolution fusion | flops 19327352832 | bytes 41943040 | tf_op jit(solution)/shard_map/dot_general | solution.py:418
  1430.9 38.5 %add_add_fusion = f32[4608,1024]{1,0:T(8,128)} fusion(f32[4608,1024]{1,0:T(8,128)} %fusion.38, f32[4608,1024]{1,0:T(8,128)} %fusion.36, f32[4608,1024]{1,0:T(8,128)} %fusion.37, bf16[2048,4608]{1,0:T(8,128)(2,1)} %all-gather.9.cloned.1.call-done.a_ref, bf16[2048,1024]{1,0:T(8,128)(2,1)} %attn_bwd.4), kind=kOutput, calls=%fused_computation.8 | convolution fusion | flops 19341508608 | bytes 98566144 | tf_op jit(solution)/shard_map/dot_general | solution.py:418
  1481.6 18.4 %copy.77 = f32[4608,2,128]{2,1,0:T(2,128)} copy(f32[4608,2,128]{2,0,1:T(8,128)S(1)} %pad_maximum_fusion.2) | data formatting | bytes 9437184
  1500.4 18.0 %copy.76 = f32[4608,2,128]{2,1,0:T(2,128)} copy(f32[4608,2,128]{2,0,1:T(8,128)S(1)} %pad_maximum_fusion.1) | data formatting | bytes 9437184
  1519.0 20.8 %copy.75 = f32[4608,4,128]{2,1,0:T(4,128)} copy(f32[4608,4,128]{2,0,1:T(8,128)S(1)} %pad_maximum_fusion) | data formatting | bytes 18874368
  1539.8 16.5 fusion.41
  1556.3 16.4 fusion.40
  1572.7 16.5 fusion.39
  1589.2 23.6 %add_add_fusion.1 = f32[512,4608]{1,0:T(8,128)} fusion(f32[512,4608]{1,0:T(8,128)} %fusion.41, f32[512,4608]{1,0:T(8,128)} %fusion.39, f32[512,4608]{1,0:T(8,128)} %fusion.40, bf16[2048,512]{1,0:T(8,128)(2,1)S(1)} %copy-done.9, bf16[2048,4608]{1,0:T(8,128)(2,1)} %all-gather.17.cloned.1.call-done), kind=kOutput, calls=%fused_computation.10 | convolution fusion | flops 9670754304 | bytes 58720256 | tf_op jit(solution)/shard_map/dot_general | solution.py:416
  1649.6 88.7 %reduce-scatter.17.cloned.1.call-done.refs_0_ = bf16[256,4608]{1,0:T(8,128)(2,1)} async-done(((bf16[2048,4608]{1,0:T(8,128)(2,1)}), bf16[256,4608]{1,0:T(8,128)(2,1)}) %reduce-scatter.17.cloned.1.call-update) | async-done | bytes 2359312 | tf_op jit(solution)/shard_map/reduce_scatter | solution.py:411
  1750.5 23.4 %all-reduce = (f32[4608]{0:T(1024)}, f32[4608]{0:T(1024)}) all-reduce(f32[4608]{0:T(1024)S(1)} %add_reduce_fusion.1, f32[4608]{0:T(1024)S(1)} %copy-done.62), channel_id=1, replica_groups=mesh['dp'=1,'tp'=8] {'tp'}, use_global_device_ids=true, to_apply=%region_13.0 | all-reduce | flops 9216 | bytes 73728 | tf_op jit(solution)/shard_map/psum | solution.py:424
  (242 shorter events, 211.4 us)
Async XLA Ops:
  7.2 101.7 %all-gather.15.cloned.1.call-start = ((), (), s32[]{:S(2)}) async-start(), calls=%async_computation.14 | async-start | bytes 21233664 | tf_op jit(solution)/shard_map/all_gather | solution.py:388
  12.2 192.0 %all-gather.13.cloned.1.call-start = ((), (), s32[]{:S(2)}) async-start(), calls=%async_computation.12 | async-start | bytes 21233664 | tf_op jit(solution)/shard_map/all_gather | solution.py:388
  16.0 283.7 %all-gather.11.cloned.1.call-start = ((), (), s32[]{:S(2)}) async-start(), calls=%async_computation.10 | async-start | bytes 21233664 | tf_op jit(solution)/shard_map/all_gather | solution.py:388
  19.7 375.2 %all-gather.9.cloned.1.call-start = ((), (), s32[]{:S(2)}) async-start(), calls=%async_computation.8 | async-start | bytes 21233664 | tf_op jit(solution)/shard_map/all_gather | solution.py:388
  23.4 491.9 %reduce-scatter.15.cloned.1.call-start = ((), (), s32[]{:S(2)}) async-start(), calls=%async_computation.15 | async-start | bytes 21233664 | tf_op jit(solution)/shard_map/reduce_scatter | solution.py:402
  38.9 97.0 %copy-start.45 = (s32[1,2048]{1,0:T(1,128)}, s32[1,2048]{1,0:T(1,128)S(1)}, u32[]{:S(2)}) copy-start(s32[1,2048]{1,0:T(1,128)S(1)} %get-tuple-element.121.posr_ref) | copy-start | bytes 24580
  38.9 192.7 %copy-start.43 = (s32[1,2048]{1,0:T(1,128)}, s32[1,2048]{1,0:T(1,128)S(1)}, u32[]{:S(2)}) copy-start(s32[1,2048]{1,0:T(1,128)S(1)} %get-tuple-element.126.posr_ref) | copy-start | bytes 24580
  38.9 288.3 %copy-start.41 = (s32[1,2048]{1,0:T(1,128)}, s32[1,2048]{1,0:T(1,128)S(1)}, u32[]{:S(2)}) copy-start(s32[1,2048]{1,0:T(1,128)S(1)} %get-tuple-element.127.posr_ref) | copy-start | bytes 24580
  38.9 383.2 %copy-start.39 = (s32[1,2048]{1,0:T(1,128)}, s32[1,2048]{1,0:T(1,128)S(1)}, u32[]{:S(2)}) copy-start(s32[1,2048]{1,0:T(1,128)S(1)} %get-tuple-element.128.posr_ref) | copy-start | bytes 24580
  39.3 96.7 %copy-start.27 = (s32[2048,1]{1,0:T(8,128)}, s32[2048,1]{1,0:T(8,128)S(1)}, u32[]{:S(2)}) copy-start(s32[2048,1]{1,0:T(8,128)S(1)} %copy.70.posc_ref) | copy-start | bytes 24580
  174.0 461.9 %reduce-scatter.13.cloned.1.call-start = ((), (), s32[]{:S(2)}) async-start(), calls=%async_computation.13 | async-start | bytes 21233664 | tf_op jit(solution)/shard_map/reduce_scatter | solution.py:402
  174.4 57.2 %copy-start.33 = (s32[2048,1]{1,0:T(8,128)}, s32[2048,1]{1,0:T(8,128)S(1)}, u32[]{:S(2)}) copy-start(s32[2048,1]{1,0:T(8,128)S(1)} %copy.69.posc_ref) | copy-start | bytes 24580
  273.1 483.4 %reduce-scatter.11.cloned.1.call-start = ((), (), s32[]{:S(2)}) async-start(), calls=%async_computation.11 | async-start | bytes 21233664 | tf_op jit(solution)/shard_map/reduce_scatter | solution.py:402
  273.5 53.7 %copy-start.31 = (s32[2048,1]{1,0:T(8,128)}, s32[2048,1]{1,0:T(8,128)S(1)}, u32[]{:S(2)}) copy-start(s32[2048,1]{1,0:T(8,128)S(1)} %copy.68.posc_ref) | copy-start | bytes 24580
  365.6 511.5 %reduce-scatter.9.cloned.1.call-start = ((), (), s32[]{:S(2)}) async-start(), calls=%async_computation.9 | async-start | bytes 21233664 | tf_op jit(solution)/shard_map/reduce_scatter | solution.py:402
  366.6 55.5 %copy-start.29 = (s32[2048,1]{1,0:T(8,128)}, s32[2048,1]{1,0:T(8,128)S(1)}, u32[]{:S(2)}) copy-start(s32[2048,1]{1,0:T(8,128)S(1)} %copy.67.posc_ref) | copy-start | bytes 24580
  474.3 497.6 %all-gather.23.cloned.1.call-start = ((), (), s32[]{:S(2)}) async-start(), calls=%async_computation.22 | async-start | bytes 21233664 | tf_op jit(solution)/shard_map/all_gather | solution.py:405
  528.2 538.4 %all-gather.21.cloned.1.call-start = ((), (), s32[]{:S(2)}) async-start(), calls=%async_computation.20 | async-start | bytes 21233664 | tf_op jit(solution)/shard_map/all_gather | solution.py:405
  648.9 512.5 %all-gather.19.cloned.1.call-start = ((), (), s32[]{:S(2)}) async-start(), calls=%async_computation.18 | async-start | bytes 21233664 | tf_op jit(solution)/shard_map/all_gather | solution.py:405
  769.3 120.6 %copy-start.35 = (f32[8,4608]{1,0:T(8,128)}, f32[8,4608]{1,0:T(8,128)S(1)}, u32[]{:S(2)}) copy-start(f32[8,4608]{1,0:T(8,128)S(1)} %get-tuple-element.62) | copy-start | bytes 442372
  769.3 486.9 %all-gather.17.cloned.1.call-start = ((), (), s32[]{:S(2)}) async-start(), calls=%async_computation.16 | async-start | bytes 21233664 | tf_op jit(solution)/shard_map/all_gather | solution.py:405
  889.9 722.9 %reduce-scatter.23.cloned.1.call-start = ((), (), s32[]{:S(2)}) async-start(), calls=%async_computation.23 | async-start | bytes 21233664 | tf_op jit(solution)/shard_map/reduce_scatter | solution.py:411
  890.6 98.0 %copy-start.25 = (f32[2048,128]{1,0:T(8,128)S(1)}, f32[2048,128]{1,0:T(8,128)}, u32[]{:S(2)}) copy-start(f32[2048,128]{1,0:T(8,128)} %get-tuple-element.102.sin_ref) | copy-start | bytes 3145732
  890.6 98.0 %copy-start.26 = (f32[2048,128]{1,0:T(8,128)S(1)}, f32[2048,128]{1,0:T(8,128)}, u32[]{:S(2)}) copy-start(f32[2048,128]{1,0:T(8,128)} %get-tuple-element.144.cos_ref) | copy-start | bytes 3145732
  890.6 98.0 %copy-start.28 = (s32[2048,1]{1,0:T(8,128)S(1)}, s32[2048,1]{1,0:T(8,128)}, u32[]{:S(2)}) copy-start(s32[2048,1]{1,0:T(8,128)} %copy-done.27) | copy-start | bytes 24580
  890.6 98.0 %copy-start.46 = (s32[1,2048]{1,0:T(1,128)S(1)}, s32[1,2048]{1,0:T(1,128)}, u32[]{:S(2)}) copy-start(s32[1,2048]{1,0:T(1,128)} %copy-done.45) | copy-start | bytes 24580
  1050.4 32.6 %copy-start.23 = (f32[2048,128]{1,0:T(8,128)S(1)}, f32[2048,128]{1,0:T(8,128)}, u32[]{:S(2)}) copy-start(f32[2048,128]{1,0:T(8,128)} %get-tuple-element.104.sin_ref) | copy-start | bytes 3145732
  1050.4 32.6 %copy-start.24 = (f32[2048,128]{1,0:T(8,128)S(1)}, f32[2048,128]{1,0:T(8,128)}, u32[]{:S(2)}) copy-start(f32[2048,128]{1,0:T(8,128)} %get-tuple-element.142.cos_ref) | copy-start | bytes 3145732
  1050.4 32.6 %copy-start.34 = (s32[2048,1]{1,0:T(8,128)S(1)}, s32[2048,1]{1,0:T(8,128)}, u32[]{:S(2)}) copy-start(s32[2048,1]{1,0:T(8,128)} %copy-done.33) | copy-start | bytes 24580
  1050.5 32.6 %copy-start.44 = (s32[1,2048]{1,0:T(1,128)S(1)}, s32[1,2048]{1,0:T(1,128)}, u32[]{:S(2)}) copy-start(s32[1,2048]{1,0:T(1,128)} %copy-done.43) | copy-start | bytes 24580
  1050.5 574.5 %reduce-scatter.21.cloned.1.call-start = ((), (), s32[]{:S(2)}) async-start(), calls=%async_computation.21 | async-start | bytes 21233664 | tf_op jit(solution)/shard_map/reduce_scatter | solution.py:411
  1150.7 27.2 %copy-start.21 = (f32[2048,128]{1,0:T(8,128)S(1)}, f32[2048,128]{1,0:T(8,128)}, u32[]{:S(2)}) copy-start(f32[2048,128]{1,0:T(8,128)} %get-tuple-element.103.sin_ref) | copy-start | bytes 3145732
  1150.7 27.2 %copy-start.22 = (f32[2048,128]{1,0:T(8,128)S(1)}, f32[2048,128]{1,0:T(8,128)}, u32[]{:S(2)}) copy-start(f32[2048,128]{1,0:T(8,128)} %get-tuple-element.143.cos_ref) | copy-start | bytes 3145732
  1150.7 27.2 %copy-start.32 = (s32[2048,1]{1,0:T(8,128)S(1)}, s32[2048,1]{1,0:T(8,128)}, u32[]{:S(2)}) copy-start(s32[2048,1]{1,0:T(8,128)} %copy-done.31) | copy-start | bytes 24580
  1150.7 27.2 %copy-start.42 = (s32[1,2048]{1,0:T(1,128)S(1)}, s32[1,2048]{1,0:T(1,128)}, u32[]{:S(2)}) copy-start(s32[1,2048]{1,0:T(1,128)} %copy-done.41) | copy-start | bytes 24580
  1150.7 486.7 %reduce-scatter.19.cloned.1.call-start = ((), (), s32[]{:S(2)}) async-start(), calls=%async_computation.19 | async-start | bytes 21233664 | tf_op jit(solution)/shard_map/reduce_scatter | solution.py:411
  1241.0 497.3 %reduce-scatter.17.cloned.1.call-start = ((), (), s32[]{:S(2)}) async-start(), calls=%async_computation.17 | async-start | bytes 21233664 | tf_op jit(solution)/shard_map/reduce_scatter | solution.py:411
  1242.7 30.2 %copy-start.9 = (bf16[2048,512]{1,0:T(8,128)(2,1)S(1)}, bf16[2048,512]{1,0:T(8,128)(2,1)}, u32[]{:S(2)}) copy-start(bf16[2048,512]{1,0:T(8,128)(2,1)} %copy-done.8) | copy-start | bytes 6291460
  1242.7 30.2 %copy-start.19 = (f32[2048,128]{1,0:T(8,128)S(1)}, f32[2048,128]{1,0:T(8,128)}, u32[]{:S(2)}) copy-start(f32[2048,128]{1,0:T(8,128)} %get-tuple-element.105.sin_ref) | copy-start | bytes 3145732
  1242.7 30.2 %copy-start.40 = (s32[1,2048]{1,0:T(1,128)S(1)}, s32[1,2048]{1,0:T(1,128)}, u32[]{:S(2)}) copy-start(s32[1,2048]{1,0:T(1,128)} %copy-done.39) | copy-start | bytes 24580
  1355.6 26.5 %copy-start.69 = (bf16[2048,1024]{1,0:T(8,128)(2,1)S(1)}, bf16[2048,1024]{1,0:T(8,128)(2,1)}, u32[]{:S(2)}) copy-start(bf16[2048,1024]{1,0:T(8,128)(2,1)} %attn_bwd.6) | copy-start | bytes 12582916
  1355.6 52.0 %slice-start.2 = ((s8[18874368]{0:T(1024)(128)(4,1)}), s8[4194304]{0:T(1024)(128)(4,1)S(1)}, s32[]{:S(2)}) async-start(s8[18874368]{0:T(1024)(128)(4,1)} %bitcast.151), calls=%async_computation.26 | async-start | bytes 8388608
  1355.6 52.0 %slice-start.3 = ((s8[18874368]{0:T(1024)(128)(4,1)}), s8[4194304]{0:T(1024)(128)(4,1)S(1)}, s32[]{:S(2)}) async-start(s8[18874368]{0:T(1024)(128)(4,1)} %bitcast.151), calls=%async_computation.27 | async-start | bytes 8388608
  1355.6 52.0 %slice-start.4 = ((s8[18874368]{0:T(1024)(128)(4,1)}), s8[4194304]{0:T(1024)(128)(4,1)S(1)}, s32[]{:S(2)}) async-start(s8[18874368]{0:T(1024)(128)(4,1)} %bitcast.151), calls=%async_computation.28 | async-start | bytes 8388608
  1382.1 25.5 %slice-start.5 = ((s8[18874368]{0:T(1024)(128)(4,1)}), s8[4194304]{0:T(1024)(128)(4,1)S(1)}, s32[]{:S(2)}) async-start(s8[18874368]{0:T(1024)(128)(4,1)} %bitcast.151), calls=%async_computation.29 | async-start | bytes 8388608
  1382.1 25.5 %slice-start.6 = ((s8[18874368]{0:T(1024)(128)(4,1)}), s8[2097152]{0:T(1024)(128)(4,1)S(1)}, s32[]{:S(2)}) async-start(s8[18874368]{0:T(1024)(128)(4,1)} %bitcast.151), calls=%async_computation.30 | async-start | bytes 4194304
  1382.1 25.5 %copy-start.68 = (bf16[2048,1024]{1,0:T(8,128)(2,1)S(1)}, bf16[2048,1024]{1,0:T(8,128)(2,1)}, u32[]{:S(2)}) copy-start(bf16[2048,1024]{1,0:T(8,128)(2,1)} %attn_bwd.7) | copy-start | bytes 12582916
  1589.2 23.7 %copy-start.18 = (f32[1,4608]{1,0:T(1,128)S(1)}, f32[1,4608]{1,0:T(1,128)}, u32[]{:S(2)}) copy-start(f32[1,4608]{1,0:T(1,128)} %broadcast_in_dim.4.gain_ref.refs_3_) | copy-start | bytes 55300
  (45 other events, 252.6 us)
Sparse Core Ops, SparseCore 0:
  12.3 96.4 all-gather.14
  111.3 92.9 all-gather.12
  206.7 92.9 all-gather.10
  301.9 92.9 all-gather.8
  398.3 117.0 reduce-scatter.14
  518.8 117.0 reduce-scatter.12
  639.4 117.0 reduce-scatter.10
  760.0 117.0 reduce-scatter.8
  878.9 92.9 all-gather.22
  973.6 92.9 all-gather.20
  1068.4 93.0 all-gather.18
  1163.1 93.0 all-gather.16
  1259.7 117.0 reduce-scatter.22
  1380.2 117.0 reduce-scatter.20
  1500.7 117.0 reduce-scatter.18
  1621.2 117.0 reduce-scatter.16
